TPU v7x, 32 devices: a whole 2x2x4 slice. The times are simulated.
32 devices in a mesh: expert: 8 (over z, x), shard: 4 (over y, core).
Axes of the slice: x: 2, y: 2, z: 4, core: 2. Of those that a mesh axis runs over, the one named last changes fastest.
Arguments:
- train_down: float32 [16, 6400, 4096], P('expert', None, 'shard'), may hold values from -0.109375 to 0.109375
- router_weight: float32 [4096, 16], P('shard', 'expert'), may hold values from -0.09375 to 0.09375
- router_gain: float32 [4096], P('shard'), may hold values from 0.25 to 1.75
Outputs:
- ready_down: bfloat16 [16, 6400, 4096], P('expert', 'shard')
- scale_down: float32 [16, 6400], P('expert', 'shard')
- serve_router: bfloat16 [4096, 16], replicated
All inputs are finite; a program needn't handle non-finite values. Where the computation divides by a largest or mean magnitude, that divisor is 1e-20 or more.
Results may differ from a plain program's by a relative error of at most 0.001.
Values may be sent and summed in bfloat16 or wider, within the bound.
A program may use at most 192 MiB of HBM per device.

v0:
```python
import functools

import jax
import jax.numpy as jnp
from jax import lax
from jax.experimental import pallas as pl
from jax.experimental.pallas import tpu as pltpu
from jax.sharding import PartitionSpec as P

LANES = 128
TAIL_SPAN = 320
MIN_SPAN = 640
LEAD = 7


def rows_per_step(count, n):
    fits = [r for r in range(16, count + 1, 16) if count % r == 0 and (n * r) % LANES == 0]
    wide = [r for r in fits if n * r >= MIN_SPAN]
    return wide[0] if wide else fits[-1]


def exchange_kernel(
    n, ne, rows, tail, lead, x_hbm, weight_ref, gain_ref, *rest
):
    main_hbm, tails = rest[0], rest[1 : 1 + n]
    scale_ref, router_ref = rest[1 + n : 3 + n]
    (xbuf, narrow, own_max, seen_max, load_sem, max_send, max_recv,
     data_send, data_recv, keep_sem, router_sem) = rest[3 + n :]
    experts, all_rows, width = x_hbm.shape
    count = all_rows // n
    blocks = count // rows
    steps = experts * blocks
    groups = n * rows // LANES
    me = lax.axis_index("shard")
    mine = lax.axis_index("expert")

    def load(i, t):
        e, b = i // blocks, i % blocks
        return pltpu.make_async_copy(
            x_hbm.at[e, pl.ds(t * count + b * rows, rows), :],
            xbuf.at[i % (lead + 3), pl.ds(t * rows, rows), :],
            load_sem.at[i % (lead + 3)],
        )

    def start_load(i):
        for t in range(n):
            load(i, t).start()

    start_load(0)
    start_load(1)

    barrier = pltpu.get_barrier_semaphore()
    for k in range(1, n):
        pl.semaphore_signal(barrier, inc=1, device_id={"shard": lax.rem(me + k, n)}, device_id_type=pl.DeviceIdType.MESH)
    for k in range(1, ne):
        pl.semaphore_signal(barrier, inc=1, device_id={"expert": lax.rem(mine + k, ne)}, device_id_type=pl.DeviceIdType.MESH)

    router_ref[mine, me] = (weight_ref[...] * gain_ref[...]).astype(jnp.bfloat16)

    def local_max(i):
        @pl.when(i + 2 < steps)
        def _():
            start_load(i + 2)

        slot = i % (lead + 3)
        pltpu.make_async_copy(xbuf.at[slot], xbuf.at[slot], load_sem.at[slot]).wait()
        for g in range(groups):
            at = pl.ds(g * LANES, LANES)
            top = jnp.abs(xbuf[slot, at, 0:LANES])
            for c in range(LANES, width, LANES):
                top = jnp.maximum(top, jnp.abs(xbuf[slot, at, c : c + LANES]))
            own_max[i, :, at] = jnp.max(top.T, axis=0, keepdims=True)

    def max_copy(i, k):
        return pltpu.make_async_remote_copy(
            src_ref=own_max.at[i],
            dst_ref=seen_max.at[i, k - 1],
            send_sem=max_send.at[0],
            recv_sem=max_recv.at[i],
            device_id={"shard": lax.rem(me + k, n)},
            device_id_type=pl.DeviceIdType.MESH,
        )

    def divide(j):
        slot = j % (lead + 3)
        pltpu.make_async_copy(seen_max.at[j], seen_max.at[j], max_recv.at[j]).wait()
        full = own_max[j]
        for k in range(1, n):
            full = jnp.maximum(full, seen_max[j, k - 1])
        scale_ref[j] = full
        for g in range(groups):
            at = pl.ds(g * LANES, LANES)
            column = jnp.broadcast_to(full[:, g * LANES : (g + 1) * LANES], (LANES, LANES)).T
            for c in range(0, width, LANES):
                narrow[j, at, c : c + LANES] = (xbuf[slot, at, c : c + LANES] / column).astype(jnp.bfloat16)

    def block_of(j, k):
        target = lax.rem(me + k, n)
        return narrow.at[j, pl.ds(pl.multiple_of(target * rows, rows), rows), :]

    def send(j):
        e, b = j // blocks, j % blocks
        at = pl.ds(pl.multiple_of(b * rows, rows), rows)
        for k in range(1, n):
            pltpu.make_async_remote_copy(
                src_ref=block_of(j, k),
                dst_ref=main_hbm.at[k, e, at, :],
                send_sem=data_send.at[k],
                recv_sem=data_recv.at[k],
                device_id={"shard": lax.rem(me + k, n)},
                device_id_type=pl.DeviceIdType.MESH,
            ).start()
        pltpu.make_async_copy(block_of(j, 0), main_hbm.at[0, e, at, :], keep_sem.at[0]).start()

    def hand_over(j):
        for k in range(n):
            pltpu.make_async_copy(block_of(j, k), tails[k].at[j - (steps - tail)], keep_sem.at[1 + k]).start()

    def send_max(i):
        for k in range(1, n):
            max_copy(i, k).start()

    def dispatch(j):
        @pl.when(j < steps - tail)
        def _():
            send(j)

        @pl.when(j >= steps - tail)
        def _():
            hand_over(j)

    def opening(j, carry):
        local_max(2 * j)
        local_max(2 * j + 1)
        send_max(2 * j)
        divide(j)
        send_max(2 * j + 1)
        dispatch(j)
        return carry

    def steady(j, carry):
        @pl.when(j + lead < steps)
        def _():
            local_max(j + lead)

        divide(j)

        @pl.when(j + lead < steps)
        def _():
            send_max(j + lead)

        dispatch(j)
        return carry

    local_max(0)
    pl.semaphore_wait(barrier, n - 1 + ne - 1)
    send_max(0)
    local_max(1)
    divide(0)
    send_max(1)
    dispatch(0)
    lax.fori_loop(1, lead, opening, 0)
    lax.fori_loop(lead, steps, steady, 0)

    for k in range(1, n):
        pltpu.make_async_remote_copy(
            src_ref=router_ref.at[mine, me], dst_ref=router_ref.at[mine, me],
            send_sem=router_sem.at[0], recv_sem=router_sem.at[1],
            device_id={"shard": lax.rem(me + k, n)}, device_id_type=pl.DeviceIdType.MESH,
        ).start()
    pieces = router_ref.at[mine, 0 : n - 1]
    pltpu.make_async_copy(pieces, pieces, router_sem.at[0]).wait()
    pltpu.make_async_copy(pieces, pieces, router_sem.at[1]).wait()
    for k in range(1, ne):
        pltpu.make_async_remote_copy(
            src_ref=router_ref.at[mine], dst_ref=router_ref.at[mine],
            send_sem=router_sem.at[2], recv_sem=router_sem.at[3],
            device_id={"expert": lax.rem(mine + k, ne)}, device_id_type=pl.DeviceIdType.MESH,
        ).start()
    slabs = router_ref.at[0 : ne - 1]
    pltpu.make_async_copy(slabs, slabs, router_sem.at[2]).wait()
    pltpu.make_async_copy(slabs, slabs, router_sem.at[3]).wait()

    for _ in range(1, n):
        every = own_max
        pltpu.make_async_copy(every, every, max_send.at[0]).wait()
    for k in range(n):
        pltpu.make_async_copy(tails[k], tails[k], keep_sem.at[1 + k]).wait()
    sent = narrow.at[0 : steps - tail, 0:rows, :]
    pltpu.make_async_copy(sent, sent, keep_sem.at[0]).wait()
    for k in range(1, n):
        pltpu.make_async_copy(sent, sent, data_send.at[k]).wait()
    for k in range(1, n):
        pltpu.make_async_copy(sent, sent, data_recv.at[k]).wait()


def place_kernel(n, position, *refs):
    parts, out_ref = refs[:n], refs[-1]
    width = parts[0].shape[-1]
    for k in range(n):
        source = lax.rem(position[0] - k + n, n)
        out_ref[0, :, pl.ds(pl.multiple_of(source * width, LANES), width)] = parts[k][...].reshape(out_ref.shape[1], width)


def per_device(n, ne, train_down, router_weight, router_gain):
    experts, all_rows, width = train_down.shape
    count = all_rows // n
    rows = rows_per_step(count, n)
    blocks = count // rows
    steps = experts * blocks
    lead = min(LEAD, steps // 2)
    tail = min(max(1, TAIL_SPAN // rows), blocks)
    depth, columns = router_weight.shape
    bf16, f32 = jnp.bfloat16, jnp.float32
    hbm = pl.BlockSpec(memory_space=pl.ANY)
    vmem = pl.BlockSpec(memory_space=pltpu.VMEM)
    dma = pltpu.SemaphoreType.DMA
    results = pl.pallas_call(
        functools.partial(exchange_kernel, n, ne, rows, tail, lead),
        out_shape=[jax.ShapeDtypeStruct((n, experts, count, width), bf16)]
        + [jax.ShapeDtypeStruct((tail, rows, width), bf16)] * n
        + [
            jax.ShapeDtypeStruct((steps, 1, n * rows), f32),
            jax.ShapeDtypeStruct((ne, n, columns, depth), bf16),
        ],
        in_specs=[hbm, vmem, vmem],
        out_specs=[hbm] * (n + 1) + [vmem, vmem],
        scratch_shapes=[
            pltpu.VMEM((lead + 3, n * rows, width), f32),
            pltpu.VMEM((steps, n * rows, width), bf16),
            pltpu.VMEM((steps, 1, n * rows), f32),
            pltpu.VMEM((steps, n - 1, 1, n * rows), f32),
            dma((lead + 3,)),
            dma((1,)),
            dma((steps,)),
            dma((n,)),
            dma((n,)),
            dma((n + 1,)),
            dma((4,)),
        ],
        compiler_params=pltpu.CompilerParams(
            collective_id=0, has_side_effects=True, vmem_limit_bytes=60 * 1024 * 1024
        ),
        name="exchange",
    )(train_down, router_weight.T, router_gain[None, :])
    main, tails, scales, router = results[0], results[1 : 1 + n], results[1 + n], results[2 + n]

    moved = [tails[0]] + [
        lax.ppermute(tails[k], "shard", [(s, (s + k) % n) for s in range(n)]) for k in range(1, n)
    ]
    position = lax.axis_index("shard").astype(jnp.int32)[None]
    done = steps - tail

    def spot(i, position):
        return (i // blocks, i % blocks, 0)

    def part_spec(k):
        return pl.BlockSpec((1, 1, rows, width), lambda i, position: (k, i // blocks, i % blocks, 0))

    ready_shape = jax.ShapeDtypeStruct((experts, count, n * width), bf16)
    ready = pl.pallas_call(
        functools.partial(place_kernel, n),
        out_shape=ready_shape,
        grid_spec=pltpu.PrefetchScalarGridSpec(
            num_scalar_prefetch=1,
            grid=(done,),
            in_specs=[part_spec(k) for k in range(n)],
            out_specs=pl.BlockSpec((1, rows, n * width), spot),
        ),
        cost_estimate=pl.CostEstimate(flops=0, bytes_accessed=4 * done * n * rows * width, transcendentals=0),
        name="place_main",
    )(position, *([main] * n))

    ready_down = pl.pallas_call(
        functools.partial(place_kernel, n),
        out_shape=ready_shape,
        grid_spec=pltpu.PrefetchScalarGridSpec(
            num_scalar_prefetch=1,
            grid=(tail,),
            in_specs=[pl.BlockSpec((1, rows, width), lambda i, position: (i, 0, 0))] * n
            + [pl.BlockSpec(memory_space=pl.ANY)],
            out_specs=pl.BlockSpec((1, rows, n * width), lambda i, position: spot(i + done, position)),
        ),
        input_output_aliases={n + 1: 0},
        cost_estimate=pl.CostEstimate(flops=0, bytes_accessed=4 * tail * n * rows * width, transcendentals=0),
        name="place_tail",
    )(position, *moved, ready)

    by_target = scales.reshape(experts, blocks, n, rows)
    scale_down = lax.dynamic_index_in_dim(by_target, position[0], 2, keepdims=False).reshape(experts, count)
    serve_router = router.transpose(0, 2, 1, 3).reshape(ne * columns, n * depth).T
    return (ready_down, scale_down, serve_router)


def solution(mesh):
    in_specs = (P("expert", None, "shard"), P("shard", "expert"), P("shard"))
    out_specs = (P("expert", "shard", None), P("expert", "shard"), P())
    return jax.shard_map(
        functools.partial(per_device, mesh.shape["shard"], mesh.shape["expert"]),
        mesh=mesh, in_specs=in_specs, out_specs=out_specs, check_vma=False,
    )
```

profile of v0, /device:TPU:0, one launch (start us, length us, event | category | flops | bytes accessed | tf_op | source)
XLA Modules:
  0.0 306.4 jit_solution(6835658476081404802)
XLA Ops:
  0.6 271.6 %exchange.1 = (bf16[4,2,1600,1024]{3,2,1,0:T(8,128)(2,1)}, bf16[2,160,1024]{2,1,0:T(8,128)(2,1)}, bf16[2,160,1024]{2,1,0:T(8,128)(2,1)}, bf16[2,160,1024]{2,1,0:...) custom-call(f32[2,6400,1024]{2,1,0:T(8,128)} %x_hbm.1, ...), custom_call_target="tpu_custom_call" | custom-call | tf_op jit(solution)/shard_map/exchange/pallas_call | solution.py:218
  272.2 0.1 collective-permute-start
  272.3 1.6 collective-permute-start.1
  273.9 1.4 collective-permute-start.2
  275.3 0.9 reduce
  276.2 0.1 reshape.16
  276.3 0.1 dynamic-slice_reduce_fusion
  276.4 0.7 reshape.17
  277.1 1.0 copy.7
  278.0 0.7 copy.8
  278.7 22.0 %place_main.1.refs_4_ = bf16[2,1600,4096]{2,1,0:T(8,128)(2,1)} custom-call(s32[1]{0:T(128)} %bitcast.position, bf16[4,2,1600,1024]{3,2,1,0:T(8,128)(2,1)} %get-tuple-element.14.refs_0_.refs_1_.refs_2_.refs_3_, bf16[4,2,1600,1024]{3,2,1,0:T(8,128)(2,1)} %get-tuple-element.14.refs_0_.refs_1_.refs_2_.refs_3_, ...), custom_call_target="tpu_custom_call" | custom-call | bytes 47185920 | tf_op jit(solution)/shard_map/place_main/pallas_call | solution.py:261
  300.7 0.0 collective-permute-done.refs_1_
  300.7 0.0 copy-start
  300.7 0.0 collective-permute-done.1.refs_2_
  300.7 0.0 copy-start.1
  300.7 2.0 collective-permute-done.2.refs_3_
  302.7 0.0 copy-start.2
  302.7 0.0 copy-done
  302.7 0.0 copy-done.1
  302.7 0.9 copy-done.2
  303.6 2.9 place_tail.1
Async XLA Ops:
  272.2 28.5 %collective-permute-start = (bf16[2,160,1024]{2,1,0:T(8,128)(2,1)}, bf16[2,160,1024]{2,1,0:T(8,128)(2,1)S(1)}, u32[]{:S(2)}, u32[]{:S(2)}) collective-permute-start(bf16[2,160,1024]{2,1,0:T(8,128)(2,1)} %get-tuple-element.11), channel_id=1, source_target_pairs={{0,1},{1,2},{2,3},{3,0},{4,5},{5,6},{6,7},{7,4},{8,9},{9,10},{10,1... | collective-permute-start | bytes 1966088 | tf_op jit(solution)/shard_map/ppermute | solution.py:249
  272.3 28.4 %collective-permute-start.1 = (bf16[2,160,1024]{2,1,0:T(8,128)(2,1)}, bf16[2,160,1024]{2,1,0:T(8,128)(2,1)S(1)}, u32[]{:S(2)}, u32[]{:S(2)}) collective-permute-start(bf16[2,160,1024]{2,1,0:T(8,128)(2,1)} %get-tuple-element.12), channel_id=1, source_target_pairs={{0,2},{1,3},{2,0},{3,1},{4,6},{5,7},{6,4},{7,5},{8,10},{9,11},{10,... | collective-permute-start | bytes 1966088 | tf_op jit(solution)/shard_map/ppermute | solution.py:249
  273.9 28.8 %collective-permute-start.2 = (bf16[2,160,1024]{2,1,0:T(8,128)(2,1)}, bf16[2,160,1024]{2,1,0:T(8,128)(2,1)S(1)}, u32[]{:S(2)}, u32[]{:S(2)}) collective-permute-start(bf16[2,160,1024]{2,1,0:T(8,128)(2,1)} %get-tuple-element.13), channel_id=1, source_target_pairs={{0,3},{1,0},{2,1},{3,2},{4,7},{5,4},{6,5},{7,6},{8,11},{9,8},{10,9... | collective-permute-start | bytes 1966088 | tf_op jit(solution)/shard_map/ppermute | solution.py:249
  300.7 2.0 copy-start
  300.7 2.0 copy-start.1
  302.7 0.9 copy-start.2
where the time goes:
time: 307 us; the launch traced here: 306 us
  Pallas kernels  296 us (96%)
  local copies, waits for them, and re-layouts  3.39 us (1%)
    pallas_call x1, Pallas kernels, per_device(): pl.pallas_call(functools.partial(exchange_kernel, n, ne, rows, tail, lead...  272 us
    pallas_call x2, Pallas kernels, per_device(): pl.pallas_call(functools.partial(place_kernel, n), out_shape=ready_shape,...  24.8 us
  transfers between devices with their start and end apart: 3, of which 1 were waited for; matrix products, arithmetic and copies ran while one was open for 1% of the time, Pallas kernels for 7%

commit v1 on v0

v1 whole, which is shorter than its diff:
```python
import functools

import jax
import jax.numpy as jnp
from jax import lax
from jax.experimental import pallas as pl
from jax.experimental.pallas import tpu as pltpu
from jax.sharding import PartitionSpec as P

LANES = 128
LEAD = 16
HEAD = 4
AHEAD = 6
HOLD = 5
DEFER = 6
TAIL_PART = 10
PLACE_ROWS = 160
RING = 16
MESH = pl.DeviceIdType.MESH


def rows_per_step(count, n):
    fits = [r for r in range(16, count + 1, 16) if count % r == 0]
    return [r for r in fits if (n * r) % LANES == 0][0]


def swap(i, k):
    for b in range(k.bit_length()):
        if (k >> b) & 1:
            i = i + (1 << b) * (1 - 2 * ((i // (1 << b)) % 2))
    return i


def exchange_kernel(n, ne, rows, done, parts, lead, head, x_hbm, weight_ref, gain_ref, *rest):
    far = range(2, n)
    main_hbm = rest[0]
    tails = [rest[1 + p * len(far) : 1 + (p + 1) * len(far)] for p in range(len(parts))]
    rest = rest[1 + len(parts) * len(far) :]
    scale_ref, router_ref = rest[:2]
    (xbuf, narrow, own_max, seen_max, load_sem, max_send, max_recv,
     data_send, data_recv, keep_sem, router_send, router_recv) = rest[2:]
    experts, all_rows, width = x_hbm.shape
    count = all_rows // n
    blocks = count // rows
    steps = experts * blocks
    slots = xbuf.shape[0]
    groups = n * rows // LANES
    me = lax.axis_index("shard")
    mine = lax.axis_index("expert")
    late = me % 2
    bits = [1 << b for b in range(ne.bit_length() - 1)]

    def load(i, t):
        e, b = i // blocks, i % blocks
        return pltpu.make_async_copy(
            x_hbm.at[e, pl.ds(t * count + b * rows, rows), :],
            xbuf.at[i % slots, pl.ds(t * rows, rows), :],
            load_sem.at[i % slots],
        )

    def start_load(i):
        for t in range(n):
            load(i, t).start()

    for i in range(min(AHEAD, steps)):
        start_load(i)

    barrier = pltpu.get_barrier_semaphore()
    for k in range(1, n):
        pl.semaphore_signal(barrier, inc=1, device_id={"shard": swap(me, k)}, device_id_type=MESH)
    for bit in bits:
        pl.semaphore_signal(barrier, inc=1, device_id={"expert": swap(mine, bit)}, device_id_type=MESH)

    router_ref[mine, me] = (weight_ref[...] * gain_ref[...]).astype(jnp.bfloat16)

    def local_max(i):
        @pl.when(i + AHEAD < steps)
        def _():
            start_load(i + AHEAD)

        slot = i % slots
        pltpu.make_async_copy(xbuf.at[slot], xbuf.at[slot], load_sem.at[slot]).wait()
        for g in range(groups):
            at = pl.ds(g * LANES, LANES)
            top = jnp.abs(xbuf[slot, at, 0:LANES])
            for c in range(LANES, width, LANES):
                top = jnp.maximum(top, jnp.abs(xbuf[slot, at, c : c + LANES]))
            own_max[i, :, at] = jnp.max(top.T, axis=0, keepdims=True)

    def send_max(i):
        for k in range(1, n):
            pltpu.make_async_remote_copy(
                src_ref=own_max.at[i],
                dst_ref=seen_max.at[i, k - 1],
                send_sem=max_send.at[0],
                recv_sem=max_recv.at[i],
                device_id={"shard": swap(me, k)},
                device_id_type=MESH,
            ).start()

    def divide(j):
        slot = j % slots
        pltpu.make_async_copy(seen_max.at[j], seen_max.at[j], max_recv.at[j]).wait()
        full = own_max[j]
        for k in range(1, n):
            full = jnp.maximum(full, seen_max[j, k - 1])
        scale_ref[j] = full
        for g in range(groups):
            at = pl.ds(g * LANES, LANES)
            column = jnp.broadcast_to(full[:, g * LANES : (g + 1) * LANES], (LANES, LANES)).T
            for c in range(0, width, LANES):
                narrow[j, at, c : c + LANES] = (xbuf[slot, at, c : c + LANES] / column).astype(jnp.bfloat16)

    def block_of(j, k):
        return narrow.at[j, pl.ds(pl.multiple_of(swap(me, k) * rows, rows), rows), :]

    def spot(j, k):
        return main_hbm.at[k, pl.ds(pl.multiple_of(j * rows, rows), rows), :]

    def push(j, k):
        pltpu.make_async_remote_copy(
            src_ref=block_of(j, k),
            dst_ref=spot(j, k),
            send_sem=data_send.at[k],
            recv_sem=data_recv.at[k],
            device_id={"shard": swap(me, k)},
            device_id_type=MESH,
        ).start()

    def push_far(j):
        for k in reversed(far):
            i = j - late * (HOLD if k % 2 else HOLD + DEFER)

            @pl.when((i >= 0) & (i < done))
            def _():
                push(i, k)

    def dispatch(j):
        push_far(j)
        if n > 1:
            push(j, 1)
        pltpu.make_async_copy(block_of(j, 0), spot(j, 0), keep_sem.at[0]).start()
        for p, (first, size) in enumerate(parts):
            @pl.when((j >= first) & (j < first + size))
            def _():
                for k in far:
                    pltpu.make_async_copy(block_of(j, k), tails[p][k - 2].at[j - first], keep_sem.at[1 + p]).start()

    def opening(j, carry):
        local_max(head + 2 * j)
        local_max(head + 2 * j + 1)
        divide(j)
        send_max(head + 2 * j)
        send_max(head + 2 * j + 1)
        dispatch(j)
        return carry

    def steady(j, carry):
        @pl.when(j + lead < steps)
        def _():
            local_max(j + lead)

        divide(j)

        @pl.when(j + lead < steps)
        def _():
            send_max(j + lead)

        dispatch(j)
        return carry

    for i in range(head):
        local_max(i)
    pl.semaphore_wait(barrier, n - 1 + len(bits))
    for i in range(head):
        send_max(i)
    for k in range(1, n):
        pltpu.make_async_remote_copy(
            src_ref=router_ref.at[mine, me], dst_ref=router_ref.at[mine, me],
            send_sem=router_send.at[0], recv_sem=router_recv.at[0],
            device_id={"shard": swap(me, k)}, device_id_type=MESH,
        ).start()
    lax.fori_loop(0, lead - head, opening, 0)

    pieces = router_ref.at[mine, 0 : n - 1]
    pltpu.make_async_copy(pieces, pieces, router_send.at[0]).wait()
    pltpu.make_async_copy(pieces, pieces, router_recv.at[0]).wait()
    for b, bit in enumerate(bits):
        held = router_ref.at[pl.ds(mine - mine % bit, bit)]
        pltpu.make_async_remote_copy(
            src_ref=held, dst_ref=held,
            send_sem=router_send.at[1 + b], recv_sem=router_recv.at[1 + b],
            device_id={"expert": swap(mine, bit)}, device_id_type=MESH,
        ).start()
        pltpu.make_async_copy(held, held, router_send.at[1 + b]).wait()
        pltpu.make_async_copy(held, held, router_recv.at[1 + b]).wait()

    lax.fori_loop(lead - head, steps, steady, 0)
    for j in range(steps, done + HOLD + DEFER):
        push_far(j)

    for _ in range(1, n):
        pltpu.make_async_copy(own_max, own_max, max_send.at[0]).wait()
    for p in range(len(parts)):
        for k in far:
            pltpu.make_async_copy(tails[p][k - 2], tails[p][k - 2], keep_sem.at[1 + p]).wait()
    every = narrow.at[0:steps, 0:rows, :]
    sent = narrow.at[0:done, 0:rows, :]
    pltpu.make_async_copy(every, every, keep_sem.at[0]).wait()
    for k in range(1, n):
        moved = sent if k in far else every
        pltpu.make_async_copy(moved, moved, data_send.at[k]).wait()
        pltpu.make_async_copy(moved, moved, data_recv.at[k]).wait()


def place_kernel(n, cut, tall, main_hbm, out_hbm, ring, load_sem, store_sem):
    total, width = main_hbm.shape[1:]
    me = lax.axis_index("shard")
    near = min(2, n)
    first = n * (cut // tall)
    chunks = first + near * ((total - cut) // tall)
    slots = ring.shape[0]
    behind = slots // 2

    def where(t):
        early = t < first
        u = t - first
        k = jnp.where(early, t % n, u % near)
        row = jnp.where(early, (t // n) * tall, cut + (u // near) * tall)
        source = 0
        for q in range(n):
            source = jnp.where(k == q, swap(me, q), source)
        return k, pl.multiple_of(row, tall), pl.multiple_of(source * width, LANES)

    def load(t):
        k, row, _ = where(t)
        return pltpu.make_async_copy(main_hbm.at[k, pl.ds(row, tall), :], ring.at[t % slots], load_sem.at[t % slots])

    def store(t):
        _, row, column = where(t)
        return pltpu.make_async_copy(
            ring.at[t % slots], out_hbm.at[pl.ds(row, tall), pl.ds(column, width)], store_sem.at[t % slots]
        )

    def step(t, carry):
        @pl.when((t >= slots) & (t < chunks + slots))
        def _():
            store(t - slots).wait()

        @pl.when(t < chunks)
        def _():
            load(t).start()

        @pl.when((t >= behind) & (t < chunks + behind))
        def _():
            load(t - behind).wait()
            store(t - behind).start()

        return carry

    lax.fori_loop(0, chunks + slots, step, 0)


def finish_kernel(n, row, *refs):
    count = n - 2
    parts, out_hbm, sem = refs[:count], refs[-2], refs[-1]
    me = lax.axis_index("shard")
    size, width = parts[0].shape

    def store(k):
        column = pl.multiple_of(swap(me, k) * width, LANES)
        return pltpu.make_async_copy(
            parts[k - 2], out_hbm.at[pl.ds(row, size), pl.ds(column, width)], sem.at[k - 2]
        )

    for k in range(2, n):
        store(k).start()
    for k in range(2, n):
        store(k).wait()


def per_device(n, ne, train_down, router_weight, router_gain):
    experts, all_rows, width = train_down.shape
    count = all_rows // n
    rows = rows_per_step(count, n)
    steps = experts * (count // rows)
    total = steps * rows
    lead = min(LEAD, steps // 2)
    head = min(HEAD, lead - 1)
    tail = max(2, steps // TAIL_PART)
    done = steps - tail
    last = max(1, tail // 5)
    parts = [(done, tail - last), (steps - last, last)]
    far = range(2, n)
    depth, columns = router_weight.shape
    rounds = ne.bit_length()
    bf16, f32 = jnp.bfloat16, jnp.float32
    hbm = pl.BlockSpec(memory_space=pl.ANY)
    vmem = pl.BlockSpec(memory_space=pltpu.VMEM)
    dma = pltpu.SemaphoreType.DMA
    results = pl.pallas_call(
        functools.partial(exchange_kernel, n, ne, rows, done, parts, lead, head),
        out_shape=[jax.ShapeDtypeStruct((n, total, width), bf16)]
        + [jax.ShapeDtypeStruct((size, rows, width), bf16) for _, size in parts for _ in far]
        + [
            jax.ShapeDtypeStruct((steps, 1, n * rows), f32),
            jax.ShapeDtypeStruct((ne, n, columns, depth), bf16),
        ],
        in_specs=[hbm, vmem, vmem],
        out_specs=[hbm] * (1 + len(parts) * len(far)) + [vmem, vmem],
        scratch_shapes=[
            pltpu.VMEM((lead + AHEAD + 1, n * rows, width), f32),
            pltpu.VMEM((steps, n * rows, width), bf16),
            pltpu.VMEM((steps, 1, n * rows), f32),
            pltpu.VMEM((steps, n - 1, 1, n * rows), f32),
            dma((lead + AHEAD + 1,)),
            dma((1,)),
            dma((steps,)),
            dma((n,)),
            dma((n,)),
            dma((1 + len(parts),)),
            dma((rounds,)),
            dma((rounds,)),
        ],
        compiler_params=pltpu.CompilerParams(
            collective_id=0, has_side_effects=True, vmem_limit_bytes=60 * 1024 * 1024
        ),
        name="exchange",
    )(train_down, router_weight.T, router_gain[None, :])
    main, scales, router = results[0], results[-2], results[-1]

    moved = []
    for p, (_, size) in enumerate(parts):
        held = results[1 + p * len(far) : 1 + (p + 1) * len(far)]
        moved.append([
            lax.ppermute(held[k - 2], "shard", [(s, s ^ k) for s in range(n)]).reshape(size * rows, width)
            for k in far
        ])

    ready_shape = jax.ShapeDtypeStruct((total, n * width), bf16)
    tall = max(r for r in range(16, PLACE_ROWS + 1, 16) if (done * rows) % r == 0 and (tail * rows) % r == 0)
    ready = pl.pallas_call(
        functools.partial(place_kernel, n, done * rows, tall),
        out_shape=ready_shape,
        in_specs=[hbm],
        out_specs=hbm,
        scratch_shapes=[pltpu.VMEM((RING, tall, width), bf16), dma((RING,)), dma((RING,))],
        compiler_params=pltpu.CompilerParams(vmem_limit_bytes=44 * 1024 * 1024),
        cost_estimate=pl.CostEstimate(flops=0, bytes_accessed=4 * done * n * rows * width, transcendentals=0),
        name="place_main",
    )(main)

    for (first, size), pieces in zip(parts, moved):
        ready = pl.pallas_call(
            functools.partial(finish_kernel, n, first * rows),
            out_shape=ready_shape,
            in_specs=[vmem] * len(far) + [hbm],
            out_specs=hbm,
            scratch_shapes=[dma((len(far),))],
            input_output_aliases={len(far): 0},
            compiler_params=pltpu.CompilerParams(vmem_limit_bytes=8 * 1024 * 1024),
            cost_estimate=pl.CostEstimate(
                flops=0, bytes_accessed=4 * size * len(far) * rows * width, transcendentals=0
            ),
            name="place_tail",
        )(*pieces, ready)

    position = lax.axis_index("shard").astype(jnp.int32)
    by_target = scales.reshape(experts, count // rows, n, rows)
    scale_down = lax.dynamic_index_in_dim(by_target, position, 2, keepdims=False).reshape(experts, count)
    serve_router = router.transpose(0, 2, 1, 3).reshape(ne * columns, n * depth).T
    return (ready.reshape(experts, count, n * width), scale_down, serve_router)


def solution(mesh):
    in_specs = (P("expert", None, "shard"), P("shard", "expert"), P("shard"))
    out_specs = (P("expert", "shard", None), P("expert", "shard"), P())
    return jax.shard_map(
        functools.partial(per_device, mesh.shape["shard"], mesh.shape["expert"]),
        mesh=mesh, in_specs=in_specs, out_specs=out_specs, check_vma=False,
    )
```

time: 307 us -> 296 us (0.964)
  Pallas kernels: 296 us -> 281 us
  starting transfers between devices: 3.03 us -> 7.68 us
    pallas_call x3 -> x4, Pallas kernels: 296 us -> 281 us  [the longest x1 262 us: per_device(): pl.pallas_call(functools.partial(exchange_kernel, n, ne, rows, done, part...]
    ppermute x3 -> x4, starting transfers between devices: 3.03 us -> 7.68 us  [per_device(): lax.ppermute(held[k - 2], 'shard', [(s, s ^ k) for s in range(n)])]
  transfers between devices with their start and end apart: 3 -> 4, of which waited for: 1 -> 2; matrix products, arithmetic and copies ran while one was open for 1% -> 1% of each run, Pallas kernels for 7% -> 6%
where the time goes in v1:
time: 296 us; the launch traced here: 295 us
  Pallas kernels  281 us (95%)
  starting transfers between devices  7.68 us (3%)
  local copies, waits for them, and re-layouts  3.49 us (1%)
    pallas_call x1, Pallas kernels, per_device(): pl.pallas_call(functools.partial(exchange_kernel, n, ne, rows, done, part...  262 us
    pallas_call x1, Pallas kernels, per_device(): pl.pallas_call(functools.partial(place_kernel, n, done * rows, tall), out...  17.1 us
    ppermute x4, starting transfers between devices, per_device(): lax.ppermute(held[k - 2], 'shard', [(s, s ^ k) for s in range(n)])  7.68 us
  transfers between devices with their start and end apart: 4, of which 2 were waited for; matrix products, arithmetic and copies ran while one was open for 1% of the time, Pallas kernels for 6%

profile of v1, /device:TPU:0, one launch (start us, length us, event | category | flops | bytes accessed | tf_op | source)
XLA Modules:
  0.0 295.4 jit_solution(945463681527593615)
XLA Ops:
  0.6 262.1 %exchange.1 = (bf16[4,3200,1024]{2,1,0:T(8,128)(2,1)}, bf16[8,32,1024]{2,1,0:T(8,128)(2,1)}, bf16[8,32,1024]{2,1,0:T(8,128)(2,1)}, bf16[2,32,1024]{2,1,0:T(8,128...) custom-call(f32[2,6400,1024]{2,1,0:T(8,128)} %x_hbm.1, ...), custom_call_target="tpu_custom_call" | custom-call | tf_op jit(solution)/shard_map/exchange/pallas_call | solution.py:301
  262.8 1.6 collective-permute-start.2
  264.4 4.6 %collective-permute-start.3 = (bf16[8,32,1024]{2,1,0:T(8,128)(2,1)}, bf16[8,32,1024]{2,1,0:T(8,128)(2,1)S(1)}, u32[]{:S(2)}, u32[]{:S(2)}) collective-permute-start(bf16[8,32,1024]{2,1,0:T(8,128)(2,1)} %get-tuple-element.13), channel_id=1, source_target_pairs={{0,3},{1,2},{2,1},{3,0},{4,7},{5,6},{6,5},{7,4},{8,11},{9,10},{10,... | collective-permute-start | bytes 1572872 | tf_op jit(solution)/shard_map/ppermute | solution.py:336
  268.9 1.5 collective-permute-start
  270.5 0.0 collective-permute-start.1
  270.5 0.9 copy.8
  271.4 0.1 reshape.36
  271.5 0.1 copy.9
  271.6 0.7 reshape.37
  272.3 1.0 copy.10
  273.3 0.7 copy.11
  274.0 17.1 %place_main.1.refs_2_ = bf16[3200,4096]{1,0:T(8,128)(2,1)} custom-call(bf16[4,3200,1024]{2,1,0:T(8,128)(2,1)} %get-tuple-element.14.main_hbm), custom_call_target="tpu_custom_call" | custom-call | bytes 47185920 | tf_op jit(solution)/shard_map/place_main/pallas_call | solution.py:342
  291.1 0.0 collective-permute-done.2
  291.1 0.8 collective-permute-done.3
  291.9 1.0 place_tail.2.refs_2_
  292.9 0.0 collective-permute-done
  292.9 1.8 collective-permute-done.1
  294.7 0.7 place_tail.3
  (1 shorter events, 0.0 us)
Async XLA Ops:
  262.8 28.4 %collective-permute-start.2 = (bf16[8,32,1024]{2,1,0:T(8,128)(2,1)}, bf16[8,32,1024]{2,1,0:T(8,128)(2,1)S(1)}, u32[]{:S(2)}, u32[]{:S(2)}) collective-permute-start(bf16[8,32,1024]{2,1,0:T(8,128)(2,1)} %get-tuple-element.12), channel_id=1, source_target_pairs={{0,2},{1,3},{2,0},{3,1},{4,6},{5,7},{6,4},{7,5},{8,10},{9,11},{10,... | collective-permute-start | bytes 1572872 | tf_op jit(solution)/shard_map/ppermute | solution.py:336
  264.4 27.5 %collective-permute-start.3 = (bf16[8,32,1024]{2,1,0:T(8,128)(2,1)}, bf16[8,32,1024]{2,1,0:T(8,128)(2,1)S(1)}, u32[]{:S(2)}, u32[]{:S(2)}) collective-permute-start(bf16[8,32,1024]{2,1,0:T(8,128)(2,1)} %get-tuple-element.13), channel_id=1, source_target_pairs={{0,3},{1,2},{2,1},{3,0},{4,7},{5,6},{6,5},{7,4},{8,11},{9,10},{10,... | collective-permute-start | bytes 1572872 | tf_op jit(solution)/shard_map/ppermute | solution.py:336
  268.9 24.0 %collective-permute-start = (bf16[2,32,1024]{2,1,0:T(8,128)(2,1)}, bf16[2,32,1024]{2,1,0:T(8,128)(2,1)S(1)}, u32[]{:S(2)}, u32[]{:S(2)}) collective-permute-start(bf16[2,32,1024]{2,1,0:T(8,128)(2,1)} %get-tuple-element.10), channel_id=1, source_target_pairs={{0,2},{1,3},{2,0},{3,1},{4,6},{5,7},{6,4},{7,5},{8,10},{9,11},{10,... | collective-permute-start | bytes 393224 | tf_op jit(solution)/shard_map/ppermute | solution.py:336
  270.5 24.3 %collective-permute-start.1 = (bf16[2,32,1024]{2,1,0:T(8,128)(2,1)}, bf16[2,32,1024]{2,1,0:T(8,128)(2,1)S(1)}, u32[]{:S(2)}, u32[]{:S(2)}) collective-permute-start(bf16[2,32,1024]{2,1,0:T(8,128)(2,1)} %get-tuple-element.11), channel_id=1, source_target_pairs={{0,3},{1,2},{2,1},{3,0},{4,7},{5,6},{6,5},{7,4},{8,11},{9,10},{10,... | collective-permute-start | bytes 393224 | tf_op jit(solution)/shard_map/ppermute | solution.py:336

commit v2 on v1

--- a/solution.py
+++ b/solution.py
@@ -11,9 +11,9 @@
 LEAD = 16
 HEAD = 4
 AHEAD = 6
-HOLD = 5
-DEFER = 6
-TAIL_PART = 10
+HOLD = 4
+DEFER = 10
+TAIL_PART = 8
 PLACE_ROWS = 160
 RING = 16
 MESH = pl.DeviceIdType.MESH
@@ -37,8 +37,9 @@
     tails = [rest[1 + p * len(far) : 1 + (p + 1) * len(far)] for p in range(len(parts))]
     rest = rest[1 + len(parts) * len(far) :]
     scale_ref, router_ref = rest[:2]
-    (xbuf, narrow, own_max, seen_max, load_sem, max_send, max_recv,
-     data_send, data_recv, keep_sem, router_send, router_recv) = rest[2:]
+    (xbuf, narrow, own_max, direct_max, sib_max, chip_max, far_max, raw, raw_column, raw_narrow,
+     load_sem, max_send, direct_recv, sib_recv, far_recv, data_send, data_recv, keep_sem,
+     router_send, router_recv, raw_sem) = rest[2:]
     experts, all_rows, width = x_hbm.shape
     count = all_rows // n
     blocks = count // rows
@@ -87,23 +88,43 @@
                 top = jnp.maximum(top, jnp.abs(xbuf[slot, at, c : c + LANES]))
             own_max[i, :, at] = jnp.max(top.T, axis=0, keepdims=True)
 
-    def send_max(i):
+    def max_copy(source, target, arrival, k):
+        return pltpu.make_async_remote_copy(
+            src_ref=source, dst_ref=target, send_sem=max_send.at[0], recv_sem=arrival,
+            device_id={"shard": swap(me, k)}, device_id_type=MESH,
+        )
+
+    def send_direct(i):
         for k in range(1, n):
-            pltpu.make_async_remote_copy(
-                src_ref=own_max.at[i],
-                dst_ref=seen_max.at[i, k - 1],
-                send_sem=max_send.at[0],
-                recv_sem=max_recv.at[i],
-                device_id={"shard": swap(me, k)},
-                device_id_type=MESH,
-            ).start()
-
-    def divide(j):
-        slot = j % slots
-        pltpu.make_async_copy(seen_max.at[j], seen_max.at[j], max_recv.at[j]).wait()
+            max_copy(own_max.at[i], direct_max.at[i, k - 1], direct_recv.at[i], k).start()
+
+    def send_sibling(i):
+        max_copy(own_max.at[i], sib_max.at[i], sib_recv.at[i], 1).start()
+
+    def join_sibling(i):
+        pltpu.make_async_copy(sib_max.at[i], sib_max.at[i], sib_recv.at[i]).wait()
+        chip_max[i] = jnp.maximum(own_max[i], sib_max[i])
+
+    def send_far(i):
+        for k in range(2, n, 2):
+            max_copy(chip_max.at[i], far_max.at[i, k // 2 - 1], far_recv.at[i], k).start()
+
+    def direct_full(j):
+        pltpu.make_async_copy(direct_max.at[j], direct_max.at[j], direct_recv.at[j]).wait()
         full = own_max[j]
         for k in range(1, n):
-            full = jnp.maximum(full, seen_max[j, k - 1])
+            full = jnp.maximum(full, direct_max[j, k - 1])
+        return full
+
+    def staged_full(j):
+        pltpu.make_async_copy(far_max.at[j], far_max.at[j], far_recv.at[j]).wait()
+        full = chip_max[j]
+        for k in range(2, n, 2):
+            full = jnp.maximum(full, far_max[j, k // 2 - 1])
+        return full
+
+    def divide(j, full):
+        slot = j % slots
         scale_ref[j] = full
         for g in range(groups):
             at = pl.ds(g * LANES, LANES)
@@ -131,7 +152,7 @@
         for k in reversed(far):
             i = j - late * (HOLD if k % 2 else HOLD + DEFER)
 
-            @pl.when((i >= 0) & (i < done))
+            @pl.when((i >= (1 if k == 2 else 0)) & (i < done))
             def _():
                 push(i, k)
 
@@ -147,11 +168,18 @@
                     pltpu.make_async_copy(block_of(j, k), tails[p][k - 2].at[j - first], keep_sem.at[1 + p]).start()
 
     def opening(j, carry):
-        local_max(head + 2 * j)
-        local_max(head + 2 * j + 1)
-        divide(j)
-        send_max(head + 2 * j)
-        send_max(head + 2 * j + 1)
+        at = head + 2 * j
+        local_max(at)
+        local_max(at + 1)
+        if not (isinstance(j, int) and j == 0):
+            join_sibling(at - 2)
+            join_sibling(at - 1)
+        divide(j, direct_full(j) if isinstance(j, int) else staged_full(j))
+        send_sibling(at)
+        send_sibling(at + 1)
+        if not (isinstance(j, int) and j == 0):
+            send_far(at - 2)
+            send_far(at - 1)
         dispatch(j)
         return carry
 
@@ -160,27 +188,56 @@
         def _():
             local_max(j + lead)
 
-        divide(j)
+        @pl.when(j + lead - 2 < steps)
+        def _():
+            join_sibling(j + lead - 2)
+
+        divide(j, staged_full(j))
 
         @pl.when(j + lead < steps)
         def _():
-            send_max(j + lead)
+            send_sibling(j + lead)
+
+        @pl.when(j + lead - 2 < steps)
+        def _():
+            send_far(j + lead - 2)
 
         dispatch(j)
         return carry
+
+    def raw_copy():
+        return pltpu.make_async_remote_copy(
+            src_ref=xbuf.at[0, pl.ds(pl.multiple_of(swap(me, 2) * rows, rows), rows), :],
+            dst_ref=raw, send_sem=raw_sem.at[0], recv_sem=raw_sem.at[1],
+            device_id={"shard": swap(me, 2)}, device_id_type=MESH,
+        )
+
+    def raw_finish():
+        pltpu.make_async_copy(raw, raw, raw_sem.at[1]).wait()
+        full = scale_ref[0]
+        for g in range(groups):
+            at = pl.ds(g * LANES, LANES)
+            raw_column[at, :] = jnp.broadcast_to(full[:, g * LANES : (g + 1) * LANES], (LANES, LANES)).T
+        column = raw_column[pl.ds(pl.multiple_of(me * rows, rows), rows), :]
+        for c in range(0, width, LANES):
+            raw_narrow[:, c : c + LANES] = (raw[:, c : c + LANES] / column).astype(jnp.bfloat16)
 
     for i in range(head):
         local_max(i)
     pl.semaphore_wait(barrier, n - 1 + len(bits))
     for i in range(head):
-        send_max(i)
+        send_direct(i)
+    raw_copy().start()
     for k in range(1, n):
         pltpu.make_async_remote_copy(
             src_ref=router_ref.at[mine, me], dst_ref=router_ref.at[mine, me],
             send_sem=router_send.at[0], recv_sem=router_recv.at[0],
             device_id={"shard": swap(me, k)}, device_id_type=MESH,
         ).start()
-    lax.fori_loop(0, lead - head, opening, 0)
+    for j in range(head):
+        opening(j, 0)
+    pltpu.make_async_copy(raw, raw, raw_sem.at[0]).wait()
+    lax.fori_loop(head, lead - head, opening, 0)
 
     pieces = router_ref.at[mine, 0 : n - 1]
     pltpu.make_async_copy(pieces, pieces, router_send.at[0]).wait()
@@ -195,20 +252,28 @@
         pltpu.make_async_copy(held, held, router_send.at[1 + b]).wait()
         pltpu.make_async_copy(held, held, router_recv.at[1 + b]).wait()
 
+    raw_finish()
     lax.fori_loop(lead - head, steps, steady, 0)
+    pltpu.make_async_copy(raw_narrow, spot(0, 2), keep_sem.at[0]).start()
     for j in range(steps, done + HOLD + DEFER):
         push_far(j)
 
     for _ in range(1, n):
-        pltpu.make_async_copy(own_max, own_max, max_send.at[0]).wait()
+        some = own_max.at[0:head]
+        pltpu.make_async_copy(some, some, max_send.at[0]).wait()
+    for _ in range(n // 2):
+        some = own_max.at[head:steps]
+        pltpu.make_async_copy(some, some, max_send.at[0]).wait()
     for p in range(len(parts)):
         for k in far:
             pltpu.make_async_copy(tails[p][k - 2], tails[p][k - 2], keep_sem.at[1 + p]).wait()
     every = narrow.at[0:steps, 0:rows, :]
     sent = narrow.at[0:done, 0:rows, :]
+    scaled = narrow.at[0 : done - 1, 0:rows, :]
     pltpu.make_async_copy(every, every, keep_sem.at[0]).wait()
+    pltpu.make_async_copy(raw_narrow, raw_narrow, keep_sem.at[0]).wait()
     for k in range(1, n):
-        moved = sent if k in far else every
+        moved = every if k == 1 else scaled if k == 2 else sent
         pltpu.make_async_copy(moved, moved, data_send.at[k]).wait()
         pltpu.make_async_copy(moved, moved, data_recv.at[k]).wait()
 
@@ -286,7 +351,7 @@
     steps = experts * (count // rows)
     total = steps * rows
     lead = min(LEAD, steps // 2)
-    head = min(HEAD, lead - 1)
+    head = min(HEAD, lead // 2)
     tail = max(2, steps // TAIL_PART)
     done = steps - tail
     last = max(1, tail // 5)
@@ -312,15 +377,24 @@
             pltpu.VMEM((lead + AHEAD + 1, n * rows, width), f32),
             pltpu.VMEM((steps, n * rows, width), bf16),
             pltpu.VMEM((steps, 1, n * rows), f32),
-            pltpu.VMEM((steps, n - 1, 1, n * rows), f32),
+            pltpu.VMEM((head, n - 1, 1, n * rows), f32),
+            pltpu.VMEM((steps, 1, n * rows), f32),
+            pltpu.VMEM((steps, 1, n * rows), f32),
+            pltpu.VMEM((steps, n // 2 - 1, 1, n * rows), f32),
+            pltpu.VMEM((rows, width), f32),
+            pltpu.VMEM((n * rows, LANES), f32),
+            pltpu.VMEM((rows, width), bf16),
             dma((lead + AHEAD + 1,)),
             dma((1,)),
+            dma((head,)),
+            dma((steps,)),
             dma((steps,)),
             dma((n,)),
             dma((n,)),
             dma((1 + len(parts),)),
             dma((rounds,)),
             dma((rounds,)),
+            dma((2,)),
         ],
         compiler_params=pltpu.CompilerParams(
             collective_id=0, has_side_effects=True, vmem_limit_bytes=60 * 1024 * 1024

time: 296 us -> 293 us (0.990)
  Pallas kernels: 281 us -> 272 us
  starting transfers between devices: 7.68 us -> 11.3 us
    pallas_call x1, Pallas kernels: 262 us -> 253 us  [per_device(): pl.pallas_call(functools.partial(exchange_kernel, n, ne, rows, done, part...]
    ppermute x4, starting transfers between devices: 7.68 us -> 11.3 us  [per_device(): lax.ppermute(held[k - 2], 'shard', [(s, s ^ k) for s in range(n)])]
where the time goes in v2:
time: 293 us; the launch traced here: 292 us
  Pallas kernels  272 us (93%)
  starting transfers between devices  11.3 us (4%)
  waiting for transfers between devices  5.3 us (2%)
  local copies, waits for them, and re-layouts  3.49 us (1%)
    pallas_call x1, Pallas kernels, per_device(): pl.pallas_call(functools.partial(exchange_kernel, n, ne, rows, done, part...  253 us
    pallas_call x1, Pallas kernels, per_device(): pl.pallas_call(functools.partial(place_kernel, n, done * rows, tall), out...  17.2 us
    ppermute x4, starting transfers between devices, per_device(): lax.ppermute(held[k - 2], 'shard', [(s, s ^ k) for s in range(n)])  11.3 us
  transfers between devices with their start and end apart: 4, of which 2 were waited for; matrix products, arithmetic and copies ran while one was open for 1% of the time, Pallas kernels for 6%

profile of v2, /device:TPU:0, one launch (start us, length us, event | category | flops | bytes accessed | tf_op | source)
XLA Modules:
  0.0 292.3 jit_solution(6556729528761819854)
XLA Ops:
  0.6 252.5 %exchange.1 = (bf16[4,3200,1024]{2,1,0:T(8,128)(2,1)}, bf16[10,32,1024]{2,1,0:T(8,128)(2,1)}, bf16[10,32,1024]{2,1,0:T(8,128)(2,1)}, bf16[2,32,1024]{2,1,0:T(8,1...) custom-call(f32[2,6400,1024]{2,1,0:T(8,128)} %x_hbm.1, ...), custom_call_target="tpu_custom_call" | custom-call | tf_op jit(solution)/shard_map/exchange/pallas_call | solution.py:366
  253.2 1.3 collective-permute-start.2
  254.5 8.7 %collective-permute-start.3 = (bf16[10,32,1024]{2,1,0:T(8,128)(2,1)}, bf16[10,32,1024]{2,1,0:T(8,128)(2,1)S(1)}, u32[]{:S(2)}, u32[]{:S(2)}) collective-permute-start(bf16[10,32,1024]{2,1,0:T(8,128)(2,1)} %get-tuple-element.13), channel_id=1, source_target_pairs={{0,3},{1,2},{2,1},{3,0},{4,7},{5,6},{6,5},{7,4},{8,11},{9,10},{10,... | collective-permute-start | bytes 1966088 | tf_op jit(solution)/shard_map/ppermute | solution.py:410
  263.2 1.3 collective-permute-start
  264.4 0.0 collective-permute-start.1
  264.4 0.9 copy.8
  265.3 0.1 reshape.36
  265.5 0.1 copy.9
  265.6 0.7 reshape.37
  266.3 1.0 copy.10
  267.2 0.7 copy.11
  267.9 17.2 %place_main.1.refs_2_ = bf16[3200,4096]{1,0:T(8,128)(2,1)} custom-call(bf16[4,3200,1024]{2,1,0:T(8,128)(2,1)} %get-tuple-element.14.main_hbm), custom_call_target="tpu_custom_call" | custom-call | bytes 46137344 | tf_op jit(solution)/shard_map/place_main/pallas_call | solution.py:416
  285.2 0.0 collective-permute-done.2
  285.2 3.6 %collective-permute-done.3 = bf16[10,32,1024]{2,1,0:T(8,128)(2,1)S(1)} collective-permute-done((bf16[10,32,1024]{2,1,0:T(8,128)(2,1)}, bf16[10,32,1024]{2,1,0:T(8,128)(2,1)S(1)}, u32[]{:S(2)}, u32[]{:S(2)}) %collective-permute-start.3) | collective-permute-done | bytes 655392 | tf_op jit(solution)/shard_map/ppermute | solution.py:410
  288.7 1.1 place_tail.2.refs_2_
  289.8 0.0 collective-permute-done
  289.8 1.7 collective-permute-done.1
  291.6 0.7 place_tail.3
  (1 shorter events, 0.0 us)
Async XLA Ops:
  253.2 32.0 %collective-permute-start.2 = (bf16[10,32,1024]{2,1,0:T(8,128)(2,1)}, bf16[10,32,1024]{2,1,0:T(8,128)(2,1)S(1)}, u32[]{:S(2)}, u32[]{:S(2)}) collective-permute-start(bf16[10,32,1024]{2,1,0:T(8,128)(2,1)} %get-tuple-element.12), channel_id=1, source_target_pairs={{0,2},{1,3},{2,0},{3,1},{4,6},{5,7},{6,4},{7,5},{8,10},{9,11},{10,... | collective-permute-start | bytes 1966088 | tf_op jit(solution)/shard_map/ppermute | solution.py:410
  254.5 34.3 %collective-permute-start.3 = (bf16[10,32,1024]{2,1,0:T(8,128)(2,1)}, bf16[10,32,1024]{2,1,0:T(8,128)(2,1)S(1)}, u32[]{:S(2)}, u32[]{:S(2)}) collective-permute-start(bf16[10,32,1024]{2,1,0:T(8,128)(2,1)} %get-tuple-element.13), channel_id=1, source_target_pairs={{0,3},{1,2},{2,1},{3,0},{4,7},{5,6},{6,5},{7,4},{8,11},{9,10},{10,... | collective-permute-start | bytes 1966088 | tf_op jit(solution)/shard_map/ppermute | solution.py:410
  263.2 26.7 %collective-permute-start = (bf16[2,32,1024]{2,1,0:T(8,128)(2,1)}, bf16[2,32,1024]{2,1,0:T(8,128)(2,1)S(1)}, u32[]{:S(2)}, u32[]{:S(2)}) collective-permute-start(bf16[2,32,1024]{2,1,0:T(8,128)(2,1)} %get-tuple-element.10), channel_id=1, source_target_pairs={{0,2},{1,3},{2,0},{3,1},{4,6},{5,7},{6,4},{7,5},{8,10},{9,11},{10,... | collective-permute-start | bytes 393224 | tf_op jit(solution)/shard_map/ppermute | solution.py:410
  264.4 27.1 %collective-permute-start.1 = (bf16[2,32,1024]{2,1,0:T(8,128)(2,1)}, bf16[2,32,1024]{2,1,0:T(8,128)(2,1)S(1)}, u32[]{:S(2)}, u32[]{:S(2)}) collective-permute-start(bf16[2,32,1024]{2,1,0:T(8,128)(2,1)} %get-tuple-element.11), channel_id=1, source_target_pairs={{0,3},{1,2},{2,1},{3,0},{4,7},{5,6},{6,5},{7,4},{8,11},{9,10},{10,... | collective-permute-start | bytes 393224 | tf_op jit(solution)/shard_map/ppermute | solution.py:410

commit v3 on v2

--- a/solution.py
+++ b/solution.py
@@ -31,7 +31,7 @@
     return i
 
 
-def exchange_kernel(n, ne, rows, done, parts, lead, head, x_hbm, weight_ref, gain_ref, *rest):
+def exchange_kernel(n, ne, rows, done, parts, lead, head, x_hbm, weight_hbm, gain_hbm, *rest):
     far = range(2, n)
     main_hbm = rest[0]
     tails = [rest[1 + p * len(far) : 1 + (p + 1) * len(far)] for p in range(len(parts))]
@@ -39,7 +39,7 @@
     scale_ref, router_ref = rest[:2]
     (xbuf, narrow, own_max, direct_max, sib_max, chip_max, far_max, raw, raw_column, raw_narrow,
      load_sem, max_send, direct_recv, sib_recv, far_recv, data_send, data_recv, keep_sem,
-     router_send, router_recv, raw_sem) = rest[2:]
+     router_send, router_recv, raw_sem, weight, gain, weight_sem) = rest[2:]
     experts, all_rows, width = x_hbm.shape
     count = all_rows // n
     blocks = count // rows
@@ -72,7 +72,12 @@
     for bit in bits:
         pl.semaphore_signal(barrier, inc=1, device_id={"expert": swap(mine, bit)}, device_id_type=MESH)
 
-    router_ref[mine, me] = (weight_ref[...] * gain_ref[...]).astype(jnp.bfloat16)
+    fetch = [
+        pltpu.make_async_copy(weight_hbm, weight, weight_sem.at[0]),
+        pltpu.make_async_copy(gain_hbm, gain, weight_sem.at[1]),
+    ]
+    for copy in fetch:
+        copy.start()
 
     def local_max(i):
         @pl.when(i + AHEAD < steps)
@@ -224,6 +229,9 @@
 
     for i in range(head):
         local_max(i)
+    for copy in fetch:
+        copy.wait()
+    router_ref[mine, me] = (weight[...] * gain[...]).astype(jnp.bfloat16)
     pl.semaphore_wait(barrier, n - 1 + len(bits))
     for i in range(head):
         send_direct(i)
@@ -371,7 +379,7 @@
             jax.ShapeDtypeStruct((steps, 1, n * rows), f32),
             jax.ShapeDtypeStruct((ne, n, columns, depth), bf16),
         ],
-        in_specs=[hbm, vmem, vmem],
+        in_specs=[hbm, hbm, hbm],
         out_specs=[hbm] * (1 + len(parts) * len(far)) + [vmem, vmem],
         scratch_shapes=[
             pltpu.VMEM((lead + AHEAD + 1, n * rows, width), f32),
@@ -395,6 +403,9 @@
             dma((rounds,)),
             dma((rounds,)),
             dma((2,)),
+            pltpu.VMEM((columns, depth), f32),
+            pltpu.VMEM((1, depth), f32),
+            dma((2,)),
         ],
         compiler_params=pltpu.CompilerParams(
             collective_id=0, has_side_effects=True, vmem_limit_bytes=60 * 1024 * 1024

time: 293 us -> 292 us (level)
  no operation moved by 1% of the time
where the time goes in v3:
time: 292 us
  Pallas kernels  271 us (93%)
  starting transfers between devices  11.1 us (4%)
  waiting for transfers between devices  5.4 us (2%)
  local copies, waits for them, and re-layouts  3.49 us (1%)
    pallas_call x1, Pallas kernels, per_device(): pl.pallas_call(functools.partial(exchange_kernel, n, ne, rows, done, part...  252 us
    pallas_call x1, Pallas kernels, per_device(): pl.pallas_call(functools.partial(place_kernel, n, done * rows, tall), out...  17.2 us
    ppermute x4, starting transfers between devices, per_device(): lax.ppermute(held[k - 2], 'shard', [(s, s ^ k) for s in range(n)])  11.1 us
  transfers between devices with their start and end apart: 4, of which 2 were waited for; matrix products, arithmetic and copies ran while one was open for 1% of the time, Pallas kernels for 6%

profile of v3, /device:TPU:0, one launch (start us, length us, event | category | flops | bytes accessed | tf_op | source)
XLA Modules:
  0.0 291.7 jit_solution(3074827482600249673)
XLA Ops:
  0.6 252.0 %exchange.1 = (bf16[4,3200,1024]{2,1,0:T(8,128)(2,1)}, bf16[10,32,1024]{2,1,0:T(8,128)(2,1)}, bf16[10,32,1024]{2,1,0:T(8,128)(2,1)}, bf16[2,32,1024]{2,1,0:T(8,1...) custom-call(f32[2,6400,1024]{2,1,0:T(8,128)} %x_hbm.1, ...), custom_call_target="tpu_custom_call" | custom-call | tf_op jit(solution)/shard_map/exchange/pallas_call | solution.py:374
  252.6 1.2 collective-permute-start.2
  253.8 8.8 %collective-permute-start.3 = (bf16[10,32,1024]{2,1,0:T(8,128)(2,1)}, bf16[10,32,1024]{2,1,0:T(8,128)(2,1)S(1)}, u32[]{:S(2)}, u32[]{:S(2)}) collective-permute-start(bf16[10,32,1024]{2,1,0:T(8,128)(2,1)} %get-tuple-element.13), channel_id=1, source_target_pairs={{0,3},{1,2},{2,1},{3,0},{4,7},{5,6},{6,5},{7,4},{8,11},{9,10},{10,... | collective-permute-start | bytes 1966088 | tf_op jit(solution)/shard_map/ppermute | solution.py:421
  262.6 1.2 collective-permute-start
  263.8 0.0 collective-permute-start.1
  263.8 0.9 copy.8
  264.7 0.1 reshape.36
  264.8 0.1 copy.9
  264.9 0.7 reshape.37
  265.6 1.0 copy.10
  266.6 0.7 copy.11
  267.3 17.2 %place_main.1.refs_2_ = bf16[3200,4096]{1,0:T(8,128)(2,1)} custom-call(bf16[4,3200,1024]{2,1,0:T(8,128)(2,1)} %get-tuple-element.14.main_hbm), custom_call_target="tpu_custom_call" | custom-call | bytes 46137344 | tf_op jit(solution)/shard_map/place_main/pallas_call | solution.py:427
  284.5 0.0 collective-permute-done.2
  284.5 3.7 %collective-permute-done.3 = bf16[10,32,1024]{2,1,0:T(8,128)(2,1)S(1)} collective-permute-done((bf16[10,32,1024]{2,1,0:T(8,128)(2,1)}, bf16[10,32,1024]{2,1,0:T(8,128)(2,1)S(1)}, u32[]{:S(2)}, u32[]{:S(2)}) %collective-permute-start.3) | collective-permute-done | bytes 655392 | tf_op jit(solution)/shard_map/ppermute | solution.py:421
  288.2 1.1 place_tail.2.refs_2_
  289.3 0.0 collective-permute-done
  289.3 1.7 collective-permute-done.1
  291.0 0.7 place_tail.3
  (1 shorter events, 0.0 us)
Async XLA Ops:
  252.6 31.9 %collective-permute-start.2 = (bf16[10,32,1024]{2,1,0:T(8,128)(2,1)}, bf16[10,32,1024]{2,1,0:T(8,128)(2,1)S(1)}, u32[]{:S(2)}, u32[]{:S(2)}) collective-permute-start(bf16[10,32,1024]{2,1,0:T(8,128)(2,1)} %get-tuple-element.12), channel_id=1, source_target_pairs={{0,2},{1,3},{2,0},{3,1},{4,6},{5,7},{6,4},{7,5},{8,10},{9,11},{10,... | collective-permute-start | bytes 1966088 | tf_op jit(solution)/shard_map/ppermute | solution.py:421
  253.8 34.3 %collective-permute-start.3 = (bf16[10,32,1024]{2,1,0:T(8,128)(2,1)}, bf16[10,32,1024]{2,1,0:T(8,128)(2,1)S(1)}, u32[]{:S(2)}, u32[]{:S(2)}) collective-permute-start(bf16[10,32,1024]{2,1,0:T(8,128)(2,1)} %get-tuple-element.13), channel_id=1, source_target_pairs={{0,3},{1,2},{2,1},{3,0},{4,7},{5,6},{6,5},{7,4},{8,11},{9,10},{10,... | collective-permute-start | bytes 1966088 | tf_op jit(solution)/shard_map/ppermute | solution.py:421
  262.6 26.7 %collective-permute-start = (bf16[2,32,1024]{2,1,0:T(8,128)(2,1)}, bf16[2,32,1024]{2,1,0:T(8,128)(2,1)S(1)}, u32[]{:S(2)}, u32[]{:S(2)}) collective-permute-start(bf16[2,32,1024]{2,1,0:T(8,128)(2,1)} %get-tuple-element.10), channel_id=1, source_target_pairs={{0,2},{1,3},{2,0},{3,1},{4,6},{5,7},{6,4},{7,5},{8,10},{9,11},{10,... | collective-permute-start | bytes 393224 | tf_op jit(solution)/shard_map/ppermute | solution.py:421
  263.8 27.2 %collective-permute-start.1 = (bf16[2,32,1024]{2,1,0:T(8,128)(2,1)}, bf16[2,32,1024]{2,1,0:T(8,128)(2,1)S(1)}, u32[]{:S(2)}, u32[]{:S(2)}) collective-permute-start(bf16[2,32,1024]{2,1,0:T(8,128)(2,1)} %get-tuple-element.11), channel_id=1, source_target_pairs={{0,3},{1,2},{2,1},{3,0},{4,7},{5,6},{6,5},{7,4},{8,11},{9,10},{10,... | collective-permute-start | bytes 393224 | tf_op jit(solution)/shard_map/ppermute | solution.py:421
